TPU v7x, 32 devices: a whole 2x2x4 slice. The times are simulated.
32 devices in a mesh: expert: 4 (over y, core), tensor: 8 (over z, x).
Axes of the slice: x: 2, y: 2, z: 4, core: 2. Of those that a mesh axis runs over, the one named last changes fastest.
Arguments:
- tokens: bfloat16 [1024, 6144], P('expert'), may hold values from -6 to 6
- expert_ids: int32 [1024, 2], P('expert'), may hold values from 0 to 3, all different within a row; in each aligned block of 256 rows (0 to 255, 256 to 511, ...) at most 192 rows name the same one
- gate_weights: float32 [1024, 2], P('expert'), may hold values from 0.2 to 1
- w_gate: bfloat16 [4, 6144, 16384], P('expert', None, 'tensor'), may hold values from -0.078125 to 0.078125
- w_up: bfloat16 [4, 6144, 16384], P('expert', None, 'tensor'), may hold values from -0.078125 to 0.078125
- w_down: bfloat16 [4, 16384, 6144], P('expert', 'tensor'), may hold values from -0.0625 to 0.0625
Outputs:
- mixed: bfloat16 [1024, 6144], P(('expert', 'tensor'))
Inputs may be any that keep to these rules, and one draw needn't show every extreme that they name: `expert_ids`: each token names two different experts. Among the 256 tokens held at one index along `expert`, no expert is named by more than 192 tokens, and in some such blocks one expert is named by exactly 192.
All inputs are finite; a program needn't handle non-finite values.
Results may differ from a plain program's by a relative error of at most 0.005.
Values may be sent and summed in bfloat16 or wider, within the bound.
A program may use at most 192 MiB of HBM per device.

v0:
```python
import jax
import jax.numpy as jnp
from jax import lax
from jax.sharding import PartitionSpec as P


def body(tokens, expert_ids, gate_weights, w_gate, w_up, w_down):
    tok_rows = tokens.shape[0]
    width = tokens.shape[1]
    groups = lax.axis_size("expert")
    capacity = 3 * tok_rows // 4
    slot_count = groups * capacity
    pair_hot = (
        expert_ids[:, :, None] == jnp.arange(groups, dtype=jnp.int32)[None, None, :]
    ).astype(jnp.int32)
    flat_hot = pair_hot.reshape(2 * tok_rows, groups)
    earlier = jnp.cumsum(flat_hot, axis=0) - flat_hot
    slot_rank = jnp.sum(earlier * flat_hot, axis=1)
    slot_index = expert_ids.reshape(-1) * capacity + slot_rank
    matched = (slot_index[None, :] == jnp.arange(slot_count, dtype=jnp.int32)[:, None]).astype(
        jnp.int32
    )
    matched = matched.reshape(slot_count, tok_rows, 2)
    taken = jnp.sum(matched, axis=2)
    slot_token = jnp.sum(taken * jnp.arange(tok_rows, dtype=jnp.int32)[None, :], axis=1)
    filled = jnp.sum(taken, axis=1) > 0
    combine = jnp.sum(matched.astype(jnp.float32) * gate_weights[None, :, :], axis=2)
    outgoing = jnp.where(filled[:, None], tokens[slot_token], jnp.zeros((), jnp.bfloat16))
    outgoing = outgoing.reshape(groups, capacity, width)
    arrived = lax.all_to_all(outgoing, "expert", split_axis=0, concat_axis=0, tiled=True)
    inputs = arrived.reshape(slot_count, width)
    gate_proj = jnp.dot(inputs, w_gate[0], preferred_element_type=jnp.float32)
    up_proj = jnp.dot(inputs, w_up[0], preferred_element_type=jnp.float32)
    hidden = (jax.nn.silu(gate_proj) * up_proj).astype(jnp.bfloat16)
    down_local = w_down[0]
    partial_value = lax.dot_general(
        down_local, hidden, (((0,), (1,)), ((), ())), preferred_element_type=jnp.float32
    )
    returned = lax.all_to_all(partial_value, "expert", split_axis=1, concat_axis=1, tiled=True)
    mixed_part = jnp.dot(returned, combine, precision=lax.Precision.HIGHEST)
    summed = lax.psum_scatter(mixed_part, "tensor", scatter_dimension=1, tiled=True)
    return summed.T.astype(jnp.bfloat16)


def solution(mesh):
    placed = (
        P("expert", None),
        P("expert", None),
        P("expert", None),
        P("expert", None, "tensor"),
        P("expert", None, "tensor"),
        P("expert", "tensor", None),
    )
    return jax.shard_map(
        body, mesh=mesh, in_specs=placed, out_specs=P(("expert", "tensor"), None), check_vma=False
    )
```

profile of v0, /device:TPU:0, one launch (start us, length us, event | category | flops | bytes accessed | tf_op | source)
XLA Modules:
  0.0 570.6 jit_solution(1858369969009648385)
XLA Ops:
  6.5 1.0 copy.19
  7.5 0.1 eq.44
  7.6 0.1 eq.40
  7.8 1.2 reduce-window.6
  9.0 0.2 slice_reduce_fusion
  9.2 0.2 reduce-window.9
  9.5 0.1 reduce_sum.50
  9.8 0.7 multiply_add_fusion
  10.5 0.2 convert_reduce_fusion.1
  10.7 0.2 multiply_reduce_fusion
  10.9 0.1 copy-done.2
  11.2 8.0 %gather_fusion = bf16[768,6144]{1,0:T(8,128)(2,1)} fusion(bf16[256,6144]{1,0:T(8,128)(2,1)S(1)} %copy-done, s32[1024]{0:T(1024)S(1)} %pad_clamp_fusion), kind=kCustom, calls=%fused_computation | custom fusion | bytes 18877440 | tf_op jit(solution)/shard_map/gather | solution.py:28
  19.2 8.1 %broadcast_select_fusion = bf16[4,192,6144]{2,1,0:T(8,128)(2,1)} fusion(bf16[4,192,6144]{2,1,0:T(8,128)(2,1)} %bitcast.43, pred[4,192]{1,0:T(4,128)(4,1)S(1)} %gt.11), kind=kLoop, calls=%fused_computation.7 | loop fusion | flops 4718592 | bytes 18875136 | tf_op jit(solution)/shard_map/jit(_where)/select_n | solution.py:28
  27.3 109.4 %all_to_all.17 = bf16[4,192,6144]{2,1,0:T(8,128)(2,1)S(1)} all-to-all(bf16[4,192,6144]{2,1,0:T(8,128)(2,1)} %broadcast_select_fusion), channel_id=1, replica_groups=mesh['expert'=4,'tensor'=8] {'expert'}, dimensions={0} | all-to-all | bytes 18874368 | tf_op jit(solution)/shard_map/all_to_all | solution.py:30
  136.6 23.2 %fusion.4 = f32[768,2048]{1,0:T(8,128)S(1)} fusion(bf16[768,6144]{1,0:T(8,128)(2,1)S(1)} %bitcast.45, bf16[1,6144,2048]{2,1,0:T(8,128)(2,1)} %param.9), kind=kOutput, calls=%fused_computation.5 | convolution fusion | flops 19327352832 | bytes 40894464 | tf_op jit(solution)/shard_map/dot_general | solution.py:32
  159.8 23.7 %multiply_convert_fusion = bf16[768,2048]{1,0:T(8,128)(2,1)S(1)} fusion(f32[768,2048]{1,0:T(8,128)S(1)} %fusion.4, bf16[768,6144]{1,0:T(8,128)(2,1)S(1)} %bitcast.46, bf16[1,6144,2048]{2,1,0:T(8,128)(2,1)} %param.10), kind=kOutput, calls=%fused_computation.8 | convolution fusion | flops 19336790016 | bytes 44040192 | tf_op jit(solution)/shard_map/dot_general | solution.py:33
  183.6 25.1 %fusion = f32[768,6144]{1,0:T(8,128)} fusion(bf16[768,2048]{1,0:T(8,128)(2,1)S(1)} %multiply_convert_fusion, bf16[1,2048,6144]{2,1,0:T(8,128)(2,1)} %param.11), kind=kOutput, calls=%fused_computation.1 | convolution fusion | flops 19327352832 | bytes 47185920 | tf_op jit(solution)/shard_map/dot_general | solution.py:36
  208.7 7.5 %all-to-all-start.1 = ((f32[6144,4,192]{0,2,1:T(8,128)}), f32[6144,4,192]{0,2,1:T(8,128)}, u32[]{:S(2)}, u32[]{:S(2)}) async-start(f32[6144,4,192]{0,2,1:T(8,128)} %bitcast.44), calls=%async_computation.1 | async-start | bytes 37748736 | tf_op jit(solution)/shard_map/all_to_all | solution.py:39
  216.2 0.3 reduce-scatter.2.cloned.1.call-start
  216.5 1.2 fusion.9
  217.7 204.0 %all-to-all-done.1 = f32[6144,4,192]{0,2,1:T(8,128)} async-done(((f32[6144,4,192]{0,2,1:T(8,128)}), f32[6144,4,192]{0,2,1:T(8,128)}, u32[]{:S(2)}, u32[]{:S(2)}) %all-to-all-start.1) | async-done | bytes 18874400 | tf_op jit(solution)/shard_map/all_to_all | solution.py:39
  421.7 21.1 %fusion.15 = f32[6144,256]{0,1:T(8,128)} fusion(f32[6144,768]{0,1:T(8,128)} %bitcast.8, f32[768,256]{1,0:T(8,128)} %fusion.9), kind=kOutput, calls=%fused_computation.31 | convolution fusion | flops 14495514624 | bytes 25952256 | tf_op jit(solution)/shard_map/dot_general | solution.py:40
  442.8 119.1 %reduce-scatter.2.cloned.1.call-done = f32[6144,32]{0,1:T(8,128)} async-done(((f32[6144,256]{0,1:T(8,128)}), f32[6144,32]{0,1:T(8,128)}) %reduce-scatter.2.cloned.1.call-update) | async-done | bytes 786448 | tf_op jit(solution)/shard_map/reduce_scatter | solution.py:41
  561.9 1.9 convert_bitcast_fusion
  (18 shorter events, 0.3 us)
Async XLA Ops:
  6.5 4.6 copy-start
  10.5 0.6 copy-start.2
  208.7 7.8 %copy-start.3 = (s32[256,2]{0,1:T(2,128)S(1)}, s32[256,2]{0,1:T(2,128)}, u32[]{:S(2)}) copy-start(s32[256,2]{0,1:T(2,128)} %copy-done.2) | copy-start | bytes 6148
  208.7 7.8 %copy-start.4 = (f32[256,2]{0,1:T(2,128)S(1)}, f32[256,2]{0,1:T(2,128)}, u32[]{:S(2)}) copy-start(f32[256,2]{0,1:T(2,128)} %param.8) | copy-start | bytes 6148
  208.7 213.0 %all-to-all-start.1 = ((f32[6144,4,192]{0,2,1:T(8,128)}), f32[6144,4,192]{0,2,1:T(8,128)}, u32[]{:S(2)}, u32[]{:S(2)}) async-start(f32[6144,4,192]{0,2,1:T(8,128)} %bitcast.44), calls=%async_computation.1 | async-start | bytes 37748736 | tf_op jit(solution)/shard_map/all_to_all | solution.py:39
  216.2 345.7 %reduce-scatter.2.cloned.1.call-start = ((), (), s32[]{:S(2)}) async-start(), calls=%async_computation.3 | async-start | bytes 7077888 | tf_op jit(solution)/shard_map/reduce_scatter | solution.py:41
  421.7 142.1 %copy-start.1 = (bf16[256,6144]{1,0:T(8,128)(2,1)S(1)}, bf16[256,6144]{1,0:T(8,128)(2,1)}, u32[]{:S(2)}) copy-start(bf16[256,6144]{1,0:T(8,128)(2,1)} %param.6) | copy-start | bytes 9437188
Sparse Core Ops, SparseCore 0:
  442.9 118.9 reduce-scatter.1
where the time goes:
time: 571 us
  waiting for transfers between devices  323 us (57%)
  blocking collectives  109 us (19%)
  matrix products  93.1 us (16%)
  other arithmetic  13.9 us (2%)
  between operations  13.5 us (2%)
  local copies, waits for them, and re-layouts  9.94 us (2%)
  starting transfers between devices  7.73 us (1%)
    all_to_all x1, waiting for transfers between devices, body(): lax.all_to_all(partial_value, 'expert', split_axis=1, concat_axis=1, tile...  204 us
    reduce_scatter x1, waiting for transfers between devices, body(): lax.psum_scatter(mixed_part, 'tensor', scatter_dimension=1, tiled=True)  119 us
    all_to_all x1, blocking collectives, body(): lax.all_to_all(outgoing, 'expert', split_axis=0, concat_axis=0, tiled=True)  109 us
    dot_general x1, matrix products, body(): lax.dot_general(down_local, hidden, (((0,), (1,)), ((), ())), preferred_e...  25.1 us
    dot_general x1, matrix products, body(): up_proj = jnp.dot(inputs, w_up[0], preferred_element_type=jnp.float32)  23.7 us
    dot_general x1, matrix products, body(): gate_proj = jnp.dot(inputs, w_gate[0], preferred_element_type=jnp.float32)  23.2 us
    dot_general x1, matrix products, body(): mixed_part = jnp.dot(returned, combine, precision=lax.Precision.HIGHEST)  21.1 us
  transfers between devices with their start and end apart: 2, of which 2 were waited for; matrix products, arithmetic and copies ran while one was open for 0% of the time, Pallas kernels for 0%

commit v1 on v0

--- a/solution.py
+++ b/solution.py
@@ -36,7 +36,12 @@
     partial_value = lax.dot_general(
         down_local, hidden, (((0,), (1,)), ((), ())), preferred_element_type=jnp.float32
     )
-    returned = lax.all_to_all(partial_value, "expert", split_axis=1, concat_axis=1, tiled=True)
+    returned = jnp.concatenate(
+        lax.all_to_all(
+            jnp.stack(jnp.split(partial_value, lax.axis_size("expert"), axis=1)), "expert", 0, 0
+        ),
+        axis=1,
+    )
     mixed_part = jnp.dot(returned, combine, precision=lax.Precision.HIGHEST)
     summed = lax.psum_scatter(mixed_part, "tensor", scatter_dimension=1, tiled=True)
     return summed.T.astype(jnp.bfloat16)

time: 571 us -> 589 us (1.032)
  local copies, waits for them, and re-layouts: 9.94 us -> 19.4 us
  other arithmetic: 13.9 us -> 22.5 us
    another operation x0 -> x1, local copies, waits for them, and re-layouts: none -> 9.48 us  [body(): jnp.stack(jnp.split(partial_value, lax.axis_size('expert'), axis=1))]
    another operation x2 -> x3, other arithmetic: 1.41 us -> 10 us  [the longest x1 8.62 us: body(): jnp.stack(jnp.split(partial_value, lax.axis_size('expert'), axis=1))]
where the time goes in v1:
time: 589 us
  waiting for transfers between devices  323 us (55%)
  blocking collectives  109 us (19%)
  matrix products  93.1 us (16%)
  other arithmetic  22.5 us (4%)
  local copies, waits for them, and re-layouts  19.4 us (3%)
  between operations  13.5 us (2%)
  starting transfers between devices  7.73 us (1%)
    all_to_all x1, waiting for transfers between devices, body(): lax.all_to_all(jnp.stack(jnp.split(partial_value, lax.axis_size('expert')...  204 us
    reduce_scatter x1, waiting for transfers between devices, body(): lax.psum_scatter(mixed_part, 'tensor', scatter_dimension=1, tiled=True)  119 us
    all_to_all x1, blocking collectives, body(): lax.all_to_all(outgoing, 'expert', split_axis=0, concat_axis=0, tiled=True)  109 us
    dot_general x1, matrix products, body(): lax.dot_general(down_local, hidden, (((0,), (1,)), ((), ())), preferred_e...  25.1 us
    dot_general x1, matrix products, body(): up_proj = jnp.dot(inputs, w_up[0], preferred_element_type=jnp.float32)  23.7 us
    dot_general x1, matrix products, body(): gate_proj = jnp.dot(inputs, w_gate[0], preferred_element_type=jnp.float32)  23.2 us
    dot_general x1, matrix products, body(): mixed_part = jnp.dot(returned, combine, precision=lax.Precision.HIGHEST)  21.1 us
  transfers between devices with their start and end apart: 2, of which 2 were waited for; matrix products, arithmetic and copies ran while one was open for 0% of the time, Pallas kernels for 0%

profile of v1, /device:TPU:0, one launch (start us, length us, event | category | flops | bytes accessed | tf_op | source)
XLA Modules:
  0.0 588.7 jit_solution(2586653806536580594)
XLA Ops:
  6.5 1.0 copy.19
  7.5 0.1 eq.44
  7.8 1.2 reduce-window.6
  9.0 0.2 slice_reduce_fusion
  9.2 0.2 reduce-window.9
  9.8 0.7 multiply_add_fusion
  10.5 0.2 convert_reduce_fusion.1
  10.7 0.2 multiply_reduce_fusion
  10.9 0.1 copy-done.2
  11.2 8.0 %gather_fusion = bf16[768,6144]{1,0:T(8,128)(2,1)} fusion(bf16[256,6144]{1,0:T(8,128)(2,1)S(1)} %copy-done, s32[1024]{0:T(1024)S(1)} %pad_clamp_fusion), kind=kCustom, calls=%fused_computation | custom fusion | bytes 18877440 | tf_op jit(solution)/shard_map/gather | solution.py:28
  19.2 8.1 %broadcast_select_fusion = bf16[4,192,6144]{2,1,0:T(8,128)(2,1)} fusion(bf16[4,192,6144]{2,1,0:T(8,128)(2,1)} %bitcast.54, pred[4,192]{1,0:T(4,128)(4,1)S(1)} %gt.11), kind=kLoop, calls=%fused_computation.9 | loop fusion | flops 4718592 | bytes 18875136 | tf_op jit(solution)/shard_map/jit(_where)/select_n | solution.py:28
  27.3 109.4 %all_to_all.10 = bf16[4,192,6144]{2,1,0:T(8,128)(2,1)S(1)} all-to-all(bf16[4,192,6144]{2,1,0:T(8,128)(2,1)} %broadcast_select_fusion), channel_id=1, replica_groups=mesh['expert'=4,'tensor'=8] {'expert'}, dimensions={0} | all-to-all | bytes 18874368 | tf_op jit(solution)/shard_map/all_to_all | solution.py:30
  136.6 23.2 %fusion.4 = f32[768,2048]{1,0:T(8,128)S(1)} fusion(bf16[768,6144]{1,0:T(8,128)(2,1)S(1)} %bitcast.55, bf16[1,6144,2048]{2,1,0:T(8,128)(2,1)} %param.9), kind=kOutput, calls=%fused_computation.5 | convolution fusion | flops 19327352832 | bytes 40894464 | tf_op jit(solution)/shard_map/dot_general | solution.py:32
  159.8 23.7 %multiply_convert_fusion = bf16[768,2048]{1,0:T(8,128)(2,1)S(1)} fusion(f32[768,2048]{1,0:T(8,128)S(1)} %fusion.4, bf16[768,6144]{1,0:T(8,128)(2,1)S(1)} %bitcast.56, bf16[1,6144,2048]{2,1,0:T(8,128)(2,1)} %param.10), kind=kOutput, calls=%fused_computation.10 | convolution fusion | flops 19336790016 | bytes 44040192 | tf_op jit(solution)/shard_map/dot_general | solution.py:33
  183.6 25.1 %fusion.6 = f32[6144,768]{0,1:T(8,128)} fusion(bf16[768,2048]{1,0:T(8,128)(2,1)S(1)} %multiply_convert_fusion, bf16[1,2048,6144]{2,1,0:T(8,128)(2,1)} %param.11), kind=kOutput, calls=%fused_computation.8 | convolution fusion | flops 19327352832 | bytes 47185920 | tf_op jit(solution)/shard_map/dot_general | solution.py:36
  208.7 9.5 %slice_bitcast_fusion.3 = (f32[1,6144,192]{1,2,0:T(8,128)S(1)}, f32[1,6144,192]{1,2,0:T(8,128)S(1)}, f32[1,6144,192]{1,2,0:T(8,128)S(1)}, f32[1,6144,192]{1,2,0:T(8,128)}) fusion(f32[6144,768]{0,1:T(8,128)} %fusion.6), kind=kLoop, calls=%fused_computation.14 | loop fusion | bytes 37748736 | tf_op jit(solution)/shard_map/stack | solution.py:41
  218.2 8.6 %pad_maximum_fusion = f32[4,6144,192]{1,2,0:T(8,128)} fusion(f32[1,6144,192]{1,2,0:T(8,128)S(1)} %get-tuple-element.8, f32[1,6144,192]{1,2,0:T(8,128)S(1)} %get-tuple-element.9, f32[1,6144,192]{1,2,0:T(8,128)} %get-tuple-element.10, f32[1,6144,192]{1,2,0:T(8,128)S(1)} %get-tuple-element.7), kind=kLoop, calls=%fused_computation.7 | loop fusion | flops 14155776 | bytes 37748736 | tf_op jit(solution)/shard_map/stack | solution.py:41
  226.8 7.5 %all-to-all-start.1 = ((f32[4,6144,192]{1,2,0:T(8,128)}), f32[4,6144,192]{1,2,0:T(8,128)}, u32[]{:S(2)}, u32[]{:S(2)}) async-start(f32[4,6144,192]{1,2,0:T(8,128)} %pad_maximum_fusion), calls=%async_computation.1 | async-start | bytes 37748736 | tf_op jit(solution)/shard_map/all_to_all | solution.py:40
  234.3 0.3 reduce-scatter.2.cloned.1.call-start
  234.6 1.2 fusion.12
  235.8 204.0 %all-to-all-done.1 = f32[4,6144,192]{1,2,0:T(8,128)} async-done(((f32[4,6144,192]{1,2,0:T(8,128)}), f32[4,6144,192]{1,2,0:T(8,128)}, u32[]{:S(2)}, u32[]{:S(2)}) %all-to-all-start.1) | async-done | bytes 18874400 | tf_op jit(solution)/shard_map/all_to_all | solution.py:40
  439.8 21.1 %fusion.18 = f32[6144,256]{0,1:T(8,128)} fusion(f32[6144,768]{0,1:T(8,128)} %bitcast.12, f32[768,256]{1,0:T(8,128)} %fusion.12), kind=kOutput, calls=%fused_computation.37 | convolution fusion | flops 14495514624 | bytes 25952256 | tf_op jit(solution)/shard_map/dot_general | solution.py:45
  460.9 119.1 %reduce-scatter.2.cloned.1.call-done = f32[6144,32]{0,1:T(8,128)} async-done(((f32[6144,256]{0,1:T(8,128)}), f32[6144,32]{0,1:T(8,128)}) %reduce-scatter.2.cloned.1.call-update) | async-done | bytes 786448 | tf_op jit(solution)/shard_map/reduce_scatter | solution.py:46
  580.0 1.9 convert_bitcast_fusion
  (20 shorter events, 0.6 us)
Async XLA Ops:
  6.5 4.6 copy-start
  10.5 0.6 copy-start.2
  226.8 7.8 %copy-start.3 = (s32[256,2]{0,1:T(2,128)S(1)}, s32[256,2]{0,1:T(2,128)}, u32[]{:S(2)}) copy-start(s32[256,2]{0,1:T(2,128)} %copy-done.2) | copy-start | bytes 6148
  226.8 7.8 %copy-start.4 = (f32[256,2]{0,1:T(2,128)S(1)}, f32[256,2]{0,1:T(2,128)}, u32[]{:S(2)}) copy-start(f32[256,2]{0,1:T(2,128)} %param.8) | copy-start | bytes 6148
  226.8 213.0 %all-to-all-start.1 = ((f32[4,6144,192]{1,2,0:T(8,128)}), f32[4,6144,192]{1,2,0:T(8,128)}, u32[]{:S(2)}, u32[]{:S(2)}) async-start(f32[4,6144,192]{1,2,0:T(8,128)} %pad_maximum_fusion), calls=%async_computation.1 | async-start | bytes 37748736 | tf_op jit(solution)/shard_map/all_to_all | solution.py:40
  234.3 345.7 %reduce-scatter.2.cloned.1.call-start = ((), (), s32[]{:S(2)}) async-start(), calls=%async_computation.3 | async-start | bytes 7077888 | tf_op jit(solution)/shard_map/reduce_scatter | solution.py:46
  439.8 142.1 %copy-start.1 = (bf16[256,6144]{1,0:T(8,128)(2,1)S(1)}, bf16[256,6144]{1,0:T(8,128)(2,1)}, u32[]{:S(2)}) copy-start(bf16[256,6144]{1,0:T(8,128)(2,1)} %param.6) | copy-start | bytes 9437188
Sparse Core Ops, SparseCore 0:
  461.0 118.9 reduce-scatter.1
